TPU v7x, 512 devices: a whole 4x4x16 slice. The times are simulated.
512 devices in a mesh: cand: 16 (over y, z_hi, core), hid: 32 (over z_lo, x).
Axes of the slice: x: 4, y: 4, z: 16 (z_hi: 2, z_lo: 8; z = z_hi * 8 + z_lo), core: 2. Of those that a mesh axis runs over, the one named last changes fastest.
Arguments:
- tokens: bfloat16 [16, 256, 2048], P('cand', None, 'hid'), may hold values from -6 to 6
- cotangent: bfloat16 [16, 256, 2048], P('cand', None, 'hid'), may hold values from -6 to 6
- gate_weight: bfloat16 [2048, 8192], P('cand', 'hid'), may hold values from -0.125 to 0.125
- up_weight: bfloat16 [2048, 8192], P('cand', 'hid'), may hold values from -0.125 to 0.125
- down_weight: bfloat16 [8192, 2048], P('hid', 'cand'), may hold values from -0.125 to 0.125
- width_steps: int32 [16], P('cand'), may hold values from 1 to 8
- block_order: int32 [32], replicated, may hold values from 0 to 31, each once
Outputs:
- grad_tokens: float32 [16, 256, 2048], P('cand', None, 'hid')
- grad_gate: float32 [2048, 8192], P('cand', 'hid')
- grad_up: float32 [2048, 8192], P('cand', 'hid')
- grad_down: float32 [8192, 2048], P('hid', 'cand')
Inputs may be any that keep to these rules, and one draw needn't show every extreme that they name: Candidate c uses the first width_steps[c] * 1024 logical hidden units. `block_order`: names each of the 32 logical blocks once.
All inputs are finite; a program needn't handle non-finite values.
Results may differ from a plain program's by a relative error of at most 0.02.
Values may be sent and summed in bfloat16 or wider, within the bound.
No kernel may reach another device: no remote copies, remote signals or barrier semaphores. Data moves between devices by JAX's collectives and lax.ppermute only.
A program may use at most 64 MiB of HBM per device.

v0:
```python
import jax
import jax.numpy as jnp
from jax import lax
from jax.sharding import PartitionSpec as P

FF = 8192


def gather_turned(arrays, axis, dims):
    turned = [jnp.moveaxis(a, dim, 0) for a, dim in zip(arrays, dims)]
    widths = [t[0].size for t in turned]
    both = jnp.concatenate([t.reshape(-1, w) for t, w in zip(turned, widths)], axis=1)
    filled = lax.all_gather(both, axis, axis=0, tiled=True)
    pieces = jnp.split(filled, [sum(widths[:k]) for k in range(1, len(widths))], axis=1)
    return tuple(
        (
            jnp.moveaxis(b.reshape(-1, *t.shape[1:]), 0, dim)
            for b, t, dim in zip(pieces, turned, dims)
        )
    )


def in_one_piece(arrays, axis, dim, along):
    ends, at = ([], 0)
    for a in arrays[:-1]:
        at += a.shape[along]
        ends.append(at)
    both = jnp.concatenate(arrays, axis=along)
    return tuple(jnp.split(lax.all_gather(both, axis, axis=dim, tiled=True), ends, axis=along))


def copy_for_each(shard, axis):
    size = lax.axis_size(axis)
    return lax.all_to_all(
        jnp.broadcast_to(shard[None], (size, *shard.shape)), axis, 0, 0, tiled=True
    )


def joined_along(pieces, dim):
    shape = list(pieces.shape[1:])
    shape[dim] *= pieces.shape[0]
    return jnp.moveaxis(pieces, 0, dim).reshape(shape)


def gathered_copies(shard, axis, dim):
    pieces = copy_for_each(shard, axis)
    return joined_along(pieces, dim)


def split_up(shard, dim, size):
    shape = shard.shape
    pieces = shard.reshape(*shape[:dim], size, shape[dim] // size, *shape[dim + 1 :])
    return jnp.moveaxis(pieces, dim, 0)


def summed_on_arrival(shard, axis, dim):
    size = lax.axis_size(axis)
    pieces = lax.all_to_all(split_up(shard, dim, size), axis, 0, 0, tiled=True)
    return jnp.sum(pieces.astype(jnp.float32), axis=0)


def in_one_piece_2(arrays, axis, dim, along):
    ends, at = ([], 0)
    for a in arrays[:-1]:
        at += a.shape[along]
        ends.append(at)
    both = jnp.concatenate(arrays, axis=along)
    return tuple(
        jnp.split(lax.psum_scatter(both, axis, scatter_dimension=dim, tiled=True), ends, axis=along)
    )


def shards(tokens, cotangent, gate_weight, up_weight, down_weight, width_steps, block_order):
    inputs, upstream = gather_turned((tokens, cotangent), "hid", (2, 2))
    inputs = inputs[0]
    upstream = upstream[0]
    gate_full, up_full = in_one_piece((gate_weight, up_weight), "cand", 0, 1)
    down_full = gathered_copies(down_weight, "cand", 1)
    width = gate_weight.shape[1]
    places = jnp.arange(block_order.shape[0], dtype=jnp.int32)
    logical = jnp.sum(jnp.where(places == lax.axis_index("hid"), block_order, 0))
    active = logical * width < width_steps[0] * (FF // 8)
    keep = active.astype(jnp.float32)
    gate = jnp.dot(inputs, gate_full, preferred_element_type=jnp.float32)
    up = jnp.dot(inputs, up_full, preferred_element_type=jnp.float32)
    sig = jax.nn.sigmoid(gate)
    act = keep * gate * sig
    hidden = (act * up).astype(jnp.bfloat16)
    dhid = keep * jnp.einsum("td,fd->tf", upstream, down_full, preferred_element_type=jnp.float32)
    forward_d_up = (dhid * act).astype(jnp.bfloat16)
    forward_d_gate = (dhid * up * keep * sig * (1.0 + gate * (1.0 - sig))).astype(jnp.bfloat16)
    down_local = jnp.einsum("tf,td->fd", hidden, upstream, preferred_element_type=jnp.float32)
    down_local, d_gate, d_up = (down_local, forward_d_gate, forward_d_up)
    gate_local = jnp.einsum("td,tf->df", inputs, d_gate, preferred_element_type=jnp.float32)
    up_local = jnp.einsum("td,tf->df", inputs, d_up, preferred_element_type=jnp.float32)
    input_part = jnp.einsum("tf,df->td", d_gate, gate_full, preferred_element_type=jnp.float32)
    input_part = input_part + jnp.einsum(
        "tf,df->td", d_up, up_full, preferred_element_type=jnp.float32
    )
    gate_local, up_local, input_part = (gate_local, up_local, input_part)
    grad_tokens = summed_on_arrival(input_part[None].astype(jnp.bfloat16), "hid", 2)
    grad_gate, grad_up = tuple(
        (
            part.astype(jnp.float32)
            for part in in_one_piece_2(
                (gate_local.astype(jnp.bfloat16), up_local.astype(jnp.bfloat16)), "cand", 0, 1
            )
        )
    )
    grad_down = summed_on_arrival(down_local.astype(jnp.bfloat16), "cand", 1)
    return (grad_tokens, grad_gate, grad_up, grad_down)


def solution(mesh):
    in_specs = (
        P("cand", None, "hid"),
        P("cand", None, "hid"),
        P("cand", "hid"),
        P("cand", "hid"),
        P("hid", "cand"),
        P("cand"),
        P(),
    )
    out_specs = (P("cand", None, "hid"), P("cand", "hid"), P("cand", "hid"), P("hid", "cand"))
    return jax.shard_map(shards, mesh=mesh, in_specs=in_specs, out_specs=out_specs, check_vma=False)
```

profile of v0, /device:TPU:2, one launch (start us, length us, event | category | flops | bytes accessed | tf_op | source)
XLA Modules:
  0.0 553.6 jit_solution(2269472352284854888)
XLA Ops:
  7.2 1.5 pad_maximum_fusion.1
  8.8 1.4 pad_maximum_fusion.2
  10.3 0.9 copy.17
  11.2 1.1 broadcast_in_dim.12
  12.3 17.8 %all-to-all-start = ((bf16[16,256,128]{1,2,0:T(8,128)(2,1)}), bf16[16,256,128]{1,2,0:T(8,128)(2,1)S(1)}, u32[]{:S(2)}, u32[]{:S(2)}) async-start(bf16[16,256,128]{1,2,0:T(8,128)(2,1)} %broadcast_in_dim.12), calls=%async_computation | async-start | bytes 2097152 | tf_op jit(solution)/shard_map/all_to_all | solution.py:34
  32.1 88.1 %all-gather.5.cloned.1.call-done = bf16[2048,512]{1,0:T(8,128)(2,1)} async-done(((bf16[128,512]{1,0:T(8,128)(2,1)}), bf16[2048,512]{1,0:T(8,128)(2,1)}) %all-gather.5.cloned.1.call-update) | async-done | bytes 2097168 | tf_op jit(solution)/shard_map/all_gather | solution.py:29
  120.1 237.6 %all-gather.3.cloned.1.call-done = bf16[2048,512]{1,0:T(8,128)(2,1)} async-done(((bf16[64,512]{1,0:T(8,128)(2,1)}), bf16[2048,512]{1,0:T(8,128)(2,1)}) %all-gather.3.cloned.1.call-update) | async-done | bytes 2097168 | tf_op jit(solution)/shard_map/all_gather | solution.py:13
  357.7 2.2 fusion.4
  360.0 1.8 fusion.7
  362.5 1.2 copy.29
  363.7 1.0 copy-done.3
  364.7 4.5 all-to-all-start.2
  369.2 2.0 multiply_convert_fusion.1
  372.2 1.3 copy.18
  373.6 2.8 convolution_convert_fusion.1
  376.4 18.0 %all-to-all-done.2 = bf16[16,256,128]{2,1,0:T(8,128)(2,1)S(1)} async-done(((bf16[16,256,128]{2,1,0:T(8,128)(2,1)}), bf16[16,256,128]{2,1,0:T(8,128)(2,1)S(1)}, u32[]{:S(2)}, u32[]{:S(2)}) %all-to-all-start.2) | async-done | bytes 1048608 | tf_op jit(solution)/shard_map/all_to_all | solution.py:58
  394.4 22.8 %all-to-all-start.1 = ((bf16[32,1,256,64]{2,3,1,0:T(8,128)(2,1)}), bf16[32,1,256,64]{2,3,1,0:T(8,128)(2,1)}, u32[]{:S(2)}, u32[]{:S(2)}) async-start(bf16[32,1,256,64]{2,3,1,0:T(8,128)(2,1)} %bitcast.17), calls=%async_computation.1 | async-start | bytes 2097152 | tf_op jit(solution)/shard_map/all_to_all | solution.py:58
  417.7 1.4 pad_maximum_fusion
  419.0 2.5 copy.23
  421.6 120.1 %reduce-scatter.4.cloned.1.call-done = bf16[128,512]{1,0:T(8,128)(2,1)} async-done(((bf16[2048,512]{1,0:T(8,128)(2,1)}), bf16[128,512]{1,0:T(8,128)(2,1)}) %reduce-scatter.4.cloned.1.call-update) | async-done | bytes 131088
  541.6 0.9 fusion.11
  542.6 0.8 copy.22
  544.3 0.8 convert_reduce_fusion
  545.1 2.0 convert_reduce_fusion.1
  (29 shorter events, 4.0 us)
Async XLA Ops:
  7.2 23.6 %copy-start.4 = (s32[32]{0:T(128)S(1)}, s32[32]{0:T(128)}, u32[]{:S(2)}) copy-start(s32[32]{0:T(128)} %param.13) | copy-start | bytes 388
  7.2 113.0 %all-gather.5.cloned.1.call-start = ((), (), s32[]{:S(2)}) async-start(), calls=%async_computation.5 | async-start | bytes 2228224 | tf_op jit(solution)/shard_map/all_gather | solution.py:29
  8.8 349.0 %all-gather.3.cloned.1.call-start = ((), (), s32[]{:S(2)}) async-start(), calls=%async_computation.4 | async-start | bytes 2162688 | tf_op jit(solution)/shard_map/all_gather | solution.py:13
  12.3 351.4 %all-to-all-start = ((bf16[16,256,128]{1,2,0:T(8,128)(2,1)}), bf16[16,256,128]{1,2,0:T(8,128)(2,1)S(1)}, u32[]{:S(2)}, u32[]{:S(2)}) async-start(bf16[16,256,128]{1,2,0:T(8,128)(2,1)} %broadcast_in_dim.12), calls=%async_computation | async-start | bytes 2097152 | tf_op jit(solution)/shard_map/all_to_all | solution.py:34
  357.7 2.2 copy-start
  360.0 2.3 copy-start.5
  361.8 0.7 copy-start.6
  363.7 1.0 copy-start.3
  364.7 29.7 %all-to-all-start.2 = ((bf16[16,256,128]{2,1,0:T(8,128)(2,1)}), bf16[16,256,128]{2,1,0:T(8,128)(2,1)S(1)}, u32[]{:S(2)}, u32[]{:S(2)}) async-start(bf16[16,256,128]{2,1,0:T(8,128)(2,1)} %bitcast.49), calls=%async_computation.2 | async-start | bytes 2097152 | tf_op jit(solution)/shard_map/all_to_all | solution.py:58
  369.2 2.1 copy-start.2
  373.5 43.6 %copy-start.1 = (bf16[2048,512]{1,0:T(8,128)(2,1)S(1)}, bf16[2048,512]{1,0:T(8,128)(2,1)}, u32[]{:S(2)}) copy-start(bf16[2048,512]{1,0:T(8,128)(2,1)} %all-gather.3.cloned.1.call-done) | copy-start | bytes 6291460
  394.4 150.7 %all-to-all-start.1 = ((bf16[32,1,256,64]{2,3,1,0:T(8,128)(2,1)}), bf16[32,1,256,64]{2,3,1,0:T(8,128)(2,1)}, u32[]{:S(2)}, u32[]{:S(2)}) async-start(bf16[32,1,256,64]{2,3,1,0:T(8,128)(2,1)} %bitcast.17), calls=%async_computation.1 | async-start | bytes 2097152 | tf_op jit(solution)/shard_map/all_to_all | solution.py:58
  417.1 124.5 %reduce-scatter.4.cloned.1.call-start = ((), (), s32[]{:S(2)}) async-start(), calls=%async_computation.6 | async-start | bytes 2228224
Sparse Core Ops, SparseCore 0:
  11.8 108.2 all-gather.4
  122.8 234.8 all-gather.2
  422.7 118.8 reduce-scatter.3
where the time goes:
time: 554 us
  waiting for transfers between devices  464 us (84%)
  starting transfers between devices  45.2 us (8%)
  between operations  15.2 us (3%)
  local copies, waits for them, and re-layouts  11 us (2%)
  matrix products  10.7 us (2%)
  other arithmetic  7.75 us (1%)
    all_gather x1, waiting for transfers between devices, gather_turned(): filled = lax.all_gather(both, axis, axis=0, tiled=True)  238 us
    unnamed x4, waiting for transfers between devices  120 us
    all_gather x1, waiting for transfers between devices, in_one_piece(): lax.all_gather(both, axis, axis=dim, tiled=True)  88.1 us
    all_to_all x2, starting transfers between devices, summed_on_arrival(): pieces = lax.all_to_all(split_up(shard, dim, size), axis, 0, 0, tiled=True)  27.2 us
    all_to_all x2, waiting for transfers between devices, summed_on_arrival(): pieces = lax.all_to_all(split_up(shard, dim, size), axis, 0, 0, tiled=True)  18 us
    all_to_all x1, starting transfers between devices, copy_for_each(): lax.all_to_all(jnp.broadcast_to(shard[None], (size, *shard.shape)), axis,...  17.8 us
  transfers between devices with their start and end apart: 6, of which 4 were waited for; matrix products, arithmetic and copies ran while one was open for 4% of the time, Pallas kernels for 0%

commit v1 on v0

--- a/solution.py
+++ b/solution.py
@@ -2,15 +2,23 @@
 import jax.numpy as jnp
 from jax import lax
 from jax.sharding import PartitionSpec as P
+from jax.lax import all_to_all, axis_size
 
 FF = 8192
+
+
+def ways_recover(unit, named_axis):
+    arr_now = axis_size(named_axis)
+    o_now = jnp.stack(arr_now * [unit], 0)
+    block_last = all_to_all(o_now, axis_name=named_axis, split_axis=0, concat_axis=0)
+    return jnp.concatenate(block_last, 0)
 
 
 def gather_turned(arrays, axis, dims):
     turned = [jnp.moveaxis(a, dim, 0) for a, dim in zip(arrays, dims)]
     widths = [t[0].size for t in turned]
     both = jnp.concatenate([t.reshape(-1, w) for t, w in zip(turned, widths)], axis=1)
-    filled = lax.all_gather(both, axis, axis=0, tiled=True)
+    filled = ways_recover(both, axis)
     pieces = jnp.split(filled, [sum(widths[:k]) for k in range(1, len(widths))], axis=1)
     return tuple(
         (

time: 554 us -> 414 us (0.75)
  waiting for transfers between devices: 464 us -> 324 us
    all_gather x1 -> x0, waiting for transfers between devices: 238 us -> none  [gather_turned(): filled = lax.all_gather(both, axis, axis=0, tiled=True)]
    all_to_all x0 -> x1, waiting for transfers between devices: none -> 123 us  [ways_recover(): all_to_all(o_now, axis_name=named_axis, split_axis=0, concat_axis=0)]
    all_gather x1, waiting for transfers between devices: 88.1 us -> 0.02 us  [in_one_piece(): lax.all_gather(both, axis, axis=dim, tiled=True)]
    all_to_all x1, waiting for transfers between devices: 0.01 us -> 45.3 us  [copy_for_each(): lax.all_to_all(jnp.broadcast_to(shard[None], (size, *shard.shape)), axis,...]
    all_to_all x2, waiting for transfers between devices: 18 us -> 35.2 us  [summed_on_arrival(): pieces = lax.all_to_all(split_up(shard, dim, size), axis, 0, 0, tiled=True)]
    all_to_all x0 -> x1, starting transfers between devices: none -> 15.8 us  [ways_recover(): all_to_all(o_now, axis_name=named_axis, split_axis=0, concat_axis=0)]
    all_to_all x1, starting transfers between devices: 17.8 us -> 10.3 us  [copy_for_each(): lax.all_to_all(jnp.broadcast_to(shard[None], (size, *shard.shape)), axis,...]
    all_to_all x2, starting transfers between devices: 27.2 us -> 20.1 us  [summed_on_arrival(): pieces = lax.all_to_all(split_up(shard, dim, size), axis, 0, 0, tiled=True)]
  transfers between devices with their start and end apart: 6 -> 6, of which waited for: 4 -> 4; matrix products, arithmetic and copies ran while one was open for 4% -> 5% of each run, Pallas kernels for 0% -> 0%
where the time goes in v1:
time: 414 us; the launch traced here: 413 us
  waiting for transfers between devices  324 us (78%)
  starting transfers between devices  46.2 us (11%)
  between operations  15.5 us (4%)
  local copies, waits for them, and re-layouts  13.4 us (3%)
  matrix products  8.73 us (2%)
  other arithmetic  5.12 us (1%)
    all_to_all x1, waiting for transfers between devices, ways_recover(): all_to_all(o_now, axis_name=named_axis, split_axis=0, concat_axis=0)  123 us
    unnamed x3, waiting for transfers between devices  121 us
    all_to_all x1, waiting for transfers between devices, copy_for_each(): lax.all_to_all(jnp.broadcast_to(shard[None], (size, *shard.shape)), axis,...  45.3 us
    all_to_all x2, waiting for transfers between devices, summed_on_arrival(): pieces = lax.all_to_all(split_up(shard, dim, size), axis, 0, 0, tiled=True)  35.2 us
    all_to_all x2, starting transfers between devices, summed_on_arrival(): pieces = lax.all_to_all(split_up(shard, dim, size), axis, 0, 0, tiled=True)  20.1 us
    all_to_all x1, starting transfers between devices, ways_recover(): all_to_all(o_now, axis_name=named_axis, split_axis=0, concat_axis=0)  15.8 us
    all_to_all x1, starting transfers between devices, copy_for_each(): lax.all_to_all(jnp.broadcast_to(shard[None], (size, *shard.shape)), axis,...  10.3 us
  transfers between devices with their start and end apart: 6, of which 4 were waited for; matrix products, arithmetic and copies ran while one was open for 5% of the time, Pallas kernels for 0%

profile of v1, /device:TPU:2, one launch (start us, length us, event | category | flops | bytes accessed | tf_op | source)
XLA Modules:
  0.0 413.3 jit_solution(1728546453825842605)
XLA Ops:
  7.2 0.8 pad_maximum_fusion.2
  7.9 1.6 stack.2
  9.5 15.8 %all-to-all-start = ((bf16[32,64,512]{2,1,0:T(8,128)(2,1)}), bf16[32,64,512]{2,1,0:T(8,128)(2,1)S(1)}, u32[]{:S(2)}, u32[]{:S(2)}) async-start(bf16[32,64,512]{2,1,0:T(8,128)(2,1)} %stack.2), calls=%async_computation | async-start | bytes 4194304 | tf_op jit(solution)/shard_map/all_to_all | solution.py:13
  26.2 122.7 %all-to-all-done = bf16[32,64,512]{2,1,0:T(8,128)(2,1)S(1)} async-done(((bf16[32,64,512]{2,1,0:T(8,128)(2,1)}), bf16[32,64,512]{2,1,0:T(8,128)(2,1)S(1)}, u32[]{:S(2)}, u32[]{:S(2)}) %all-to-all-start) | async-done | bytes 2097184 | tf_op jit(solution)/shard_map/all_to_all | solution.py:13
  148.9 1.1 broadcast_in_dim.12
  150.0 10.3 %all-to-all-start.1 = ((bf16[16,256,128]{1,2,0:T(8,128)(2,1)}), bf16[16,256,128]{1,2,0:T(8,128)(2,1)S(1)}, u32[]{:S(2)}, u32[]{:S(2)}) async-start(bf16[16,256,128]{1,2,0:T(8,128)(2,1)} %broadcast_in_dim.12), calls=%async_computation.1 | async-start | bytes 2097152 | tf_op jit(solution)/shard_map/all_to_all | solution.py:42
  162.3 1.8 fusion.4
  165.4 1.2 copy.29
  166.6 45.3 %all-to-all-done.1 = bf16[16,256,128]{1,2,0:T(8,128)(2,1)S(1)} async-done(((bf16[16,256,128]{1,2,0:T(8,128)(2,1)}), bf16[16,256,128]{1,2,0:T(8,128)(2,1)S(1)}, u32[]{:S(2)}, u32[]{:S(2)}) %all-to-all-start.1) | async-done | bytes 1048608 | tf_op jit(solution)/shard_map/all_to_all | solution.py:42
  211.9 1.0 copy-done.3
  212.9 8.6 %all-to-all-start.3 = ((bf16[16,256,128]{2,1,0:T(8,128)(2,1)}), bf16[16,256,128]{2,1,0:T(8,128)(2,1)S(1)}, u32[]{:S(2)}, u32[]{:S(2)}) async-start(bf16[16,256,128]{2,1,0:T(8,128)(2,1)} %bitcast.58), calls=%async_computation.3 | async-start | bytes 2097152 | tf_op jit(solution)/shard_map/all_to_all | solution.py:66
  221.5 2.0 multiply_convert_fusion.1
  224.0 1.5 fusion
  225.5 2.3 copy.18
  227.8 1.5 convolution_convert_fusion.1
  229.2 35.2 %all-to-all-done.3 = bf16[16,256,128]{2,1,0:T(8,128)(2,1)S(1)} async-done(((bf16[16,256,128]{2,1,0:T(8,128)(2,1)}), bf16[16,256,128]{2,1,0:T(8,128)(2,1)S(1)}, u32[]{:S(2)}, u32[]{:S(2)}) %all-to-all-start.3) | async-done | bytes 1048608 | tf_op jit(solution)/shard_map/all_to_all | solution.py:66
  264.4 11.5 %all-to-all-start.2 = ((bf16[32,1,256,64]{2,3,1,0:T(8,128)(2,1)}), bf16[32,1,256,64]{2,3,1,0:T(8,128)(2,1)}, u32[]{:S(2)}, u32[]{:S(2)}) async-start(bf16[32,1,256,64]{2,3,1,0:T(8,128)(2,1)} %bitcast.57), calls=%async_computation.2 | async-start | bytes 2097152 | tf_op jit(solution)/shard_map/all_to_all | solution.py:66
  277.4 2.5 copy.23
  280.0 121.0 %reduce-scatter.4.cloned.1.call-done = bf16[128,512]{1,0:T(8,128)(2,1)} async-done(((bf16[2048,512]{1,0:T(8,128)(2,1)}), bf16[128,512]{1,0:T(8,128)(2,1)}) %reduce-scatter.4.cloned.1.call-update) | async-done | bytes 131088
  400.9 0.9 fusion.11
  401.9 0.8 copy.22
  402.8 0.8 copy.21
  403.6 0.8 convert_reduce_fusion
  404.4 2.0 convert_reduce_fusion.1
  (35 shorter events, 5.0 us)
Async XLA Ops:
  9.5 15.9 %copy-start.5 = (bf16[128,256]{1,0:T(8,128)(2,1)S(1)}, bf16[128,256]{1,0:T(8,128)(2,1)}, u32[]{:S(2)}) copy-start(bf16[128,256]{1,0:T(8,128)(2,1)} %param.10) | copy-start | bytes 196612
  9.5 15.9 %copy-start.6 = (bf16[128,256]{1,0:T(8,128)(2,1)S(1)}, bf16[128,256]{1,0:T(8,128)(2,1)}, u32[]{:S(2)}) copy-start(bf16[128,256]{1,0:T(8,128)(2,1)} %param.9) | copy-start | bytes 196612
  9.5 16.6 %copy-start.4 = (bf16[256,128]{1,0:T(8,128)(2,1)S(1)}, bf16[256,128]{1,0:T(8,128)(2,1)}, u32[]{:S(2)}) copy-start(bf16[256,128]{1,0:T(8,128)(2,1)} %param.11) | copy-start | bytes 196612
  9.5 139.4 %all-to-all-start = ((bf16[32,64,512]{2,1,0:T(8,128)(2,1)}), bf16[32,64,512]{2,1,0:T(8,128)(2,1)S(1)}, u32[]{:S(2)}, u32[]{:S(2)}) async-start(bf16[32,64,512]{2,1,0:T(8,128)(2,1)} %stack.2), calls=%async_computation | async-start | bytes 4194304 | tf_op jit(solution)/shard_map/all_to_all | solution.py:13
  25.3 135.6 %copy-start.7 = (s32[32]{0:T(128)S(1)}, s32[32]{0:T(128)}, u32[]{:S(2)}) copy-start(s32[32]{0:T(128)} %param.13) | copy-start | bytes 388
  25.3 136.9 %all-gather.2.cloned.1.call-start = ((), (), s32[]{:S(2)}) async-start(), calls=%async_computation.5 | async-start | bytes 2228224 | tf_op jit(solution)/shard_map/all_gather | solution.py:37
  150.0 61.9 %all-to-all-start.1 = ((bf16[16,256,128]{1,2,0:T(8,128)(2,1)}), bf16[16,256,128]{1,2,0:T(8,128)(2,1)S(1)}, u32[]{:S(2)}, u32[]{:S(2)}) async-start(bf16[16,256,128]{1,2,0:T(8,128)(2,1)} %broadcast_in_dim.12), calls=%async_computation.1 | async-start | bytes 2097152 | tf_op jit(solution)/shard_map/all_to_all | solution.py:42
  162.3 1.9 copy-start.1
  164.2 1.0 copy-start.8
  164.7 0.7 copy-start.9
  211.9 1.0 copy-start.3
  212.9 51.5 %all-to-all-start.3 = ((bf16[16,256,128]{2,1,0:T(8,128)(2,1)}), bf16[16,256,128]{2,1,0:T(8,128)(2,1)S(1)}, u32[]{:S(2)}, u32[]{:S(2)}) async-start(bf16[16,256,128]{2,1,0:T(8,128)(2,1)} %bitcast.58), calls=%async_computation.3 | async-start | bytes 2097152 | tf_op jit(solution)/shard_map/all_to_all | solution.py:66
  221.5 2.1 copy-start.2
  264.4 140.0 %all-to-all-start.2 = ((bf16[32,1,256,64]{2,3,1,0:T(8,128)(2,1)}), bf16[32,1,256,64]{2,3,1,0:T(8,128)(2,1)}, u32[]{:S(2)}, u32[]{:S(2)}) async-start(bf16[32,1,256,64]{2,3,1,0:T(8,128)(2,1)} %bitcast.57), calls=%async_computation.2 | async-start | bytes 2097152 | tf_op jit(solution)/shard_map/all_to_all | solution.py:66
  275.9 125.1 %reduce-scatter.4.cloned.1.call-start = ((), (), s32[]{:S(2)}) async-start(), calls=%async_computation.6 | async-start | bytes 2228224
  275.9 1.2 copy-start
Sparse Core Ops, SparseCore 0:
  30.0 98.9 all-gather.1
  281.5 119.3 reduce-scatter.3
